TPU v7x, 64 devices: a 2x2x8 block of a 4x4x8 slice. The times are simulated.
64 devices in a mesh: rep: 4 (over x, y), dp: 16 (over z, core).
Axes of the slice: x: 2, y: 2, z: 8, core: 2. Of those that a mesh axis runs over, the one named last changes fastest.
The devices are a block of a 4x4x8 slice.
Arguments:
- a: bfloat16 [64, 4, 8192, 512], P(('rep', 'dp')), parts along dimension 0
- g: bfloat16 [64, 4, 8192, 1280], P(('rep', 'dp')), parts along dimension 0
Outputs:
- output: bfloat16 [16, 512, 1280], P('rep'), parts along dimension 0
There are 4 independent parts. A program takes and returns all parts, laid end to end along the dimension named above; each array names one.
All inputs are finite; a program needn't handle non-finite values.
Results may differ from a plain program's by a relative error of at most 0.012.
Values are sent between devices in bfloat16 or wider.
A program may use at most 768 MiB of HBM per device.

v0:
```python
import jax
import jax.numpy as jnp


def solution(mesh):
    groups = mesh.shape["rep"]

    def step(a, g):
        a, g = (t.reshape(groups, -1, *t.shape[1:]) for t in (a, g))
        sums = jnp.einsum("rsntd,rsntf->rndf", a, g, preferred_element_type=jnp.float32)
        return sums.astype(jnp.bfloat16).reshape(-1, *sums.shape[2:])

    return step
```

profile of v0, /device:TPU:21, one launch (start us, length us, event | category | flops | bytes accessed | tf_op | source)
XLA Modules:
  0.0 179.9 jit_solution(12509484604841138129)
XLA Ops:
  0.0 55.4 %fusion.3 = f32[1,4,512,1280]{3,2,1,0:T(8,128)} fusion(bf16[1,4,8192,1280]{3,2,1,0:T(8,128)(2,1)} %param.1, bf16[1,4,8192,512]{3,2,1,0:T(8,128)(2,1)} %param), kind=kOutput, calls=%fused_computation.3 | convolution fusion | flops 42949672960 | bytes 127926272 | tf_op jit(solution)/rsntd,rsntf->rndf/dot_general | solution.py:10
  55.4 124.6 %all-reduce.2 = bf16[1,4,512,1280]{3,2,1,0:T(8,128)(2,1)} all-reduce(f32[1,4,512,1280]{3,2,1,0:T(8,128)} %fusion.3), channel_id=1, replica_groups=[4,16]<=[64], use_global_device_ids=true, to_apply=%add.clone | all-reduce | flops 2621440 | bytes 15728640 | tf_op jit(solution)/rsntd,rsntf->rndf/dot_general | solution.py:10
where the time goes:
time: 182 us; the launch traced here: 180 us
  blocking collectives  125 us (69%)
  matrix products  55.4 us (30%)
    dot_general x1, blocking collectives, step(): jnp.einsum('rsntd,rsntf->rndf', a, g, preferred_element_type=jnp.float32)  125 us
    dot_general x1, matrix products, step(): jnp.einsum('rsntd,rsntf->rndf', a, g, preferred_element_type=jnp.float32)  55.4 us

commit v1 on v0

v1 whole, which is shorter than its diff:
```python
import functools

import jax
import jax.numpy as jnp
from jax import lax
from jax.experimental import pallas as pl
from jax.experimental.pallas import tpu as pltpu

BF16, F32 = jnp.bfloat16, jnp.float32
COLS = 256
TOKS = 2048
DEPTH = 3
LAG = 2


def sums_kernel(chips, a_ref, g_ref, o_ref, a_in, a_t, g_in, acc, own, x_tx, x_rx, r_tx, r_rx, res,
                a_sem, g_sem, o_sem, x_send, x_recv, r_send, r_recv, q_send, q_recv, f_send, f_recv):
    mats, toks, d = a_ref.shape
    per = g_ref.shape[2] // COLS
    steps = toks // TOKS
    pieces = mats * per
    half = d // 2
    rows = half // chips
    hops = chips // 2

    rep, me = lax.axis_index("rep"), lax.axis_index("dp")
    chip, core = me // 2, lax.rem(me, 2)

    def at(z, c):
        return (rep, lax.rem(z + chips, chips) * 2 + c)

    partner, up, down = at(chip, 1 - core), at(chip + 1, core), at(chip - 1, core)
    ahead = (up, down)
    sign = (1, -1)

    barrier = pltpu.get_barrier_semaphore()
    for dev in (partner, up, down):
        pl.semaphore_signal(barrier, inc=1, device_id=dev, device_id_type=pl.DeviceIdType.MESH)
    pl.semaphore_wait(barrier, 3)

    def remote(src, dst, ss, rs, dev):
        return pltpu.make_async_remote_copy(src_ref=src, dst_ref=dst, send_sem=ss, recv_sem=rs, device_id=dev,
                                            device_id_type=pl.DeviceIdType.MESH)

    def each(lo, hi, f):
        def body(i, carry):
            f(i)
            return carry
        lax.fori_loop(lo, hi, body, 0)

    def a_copy(n, k):
        ks = pl.ds(pl.multiple_of(k * TOKS, TOKS), TOKS)
        return pltpu.make_async_copy(a_ref.at[n, ks, :], a_in.at[ks, :], a_sem.at[k])

    def g_copy(c, k):
        ks = pl.ds(pl.multiple_of(k * TOKS, TOKS), TOKS)
        cs = pl.ds(pl.multiple_of((c % per) * COLS, COLS), COLS)
        s = lax.rem(c, DEPTH)
        return pltpu.make_async_copy(g_ref.at[c // per, ks, cs], g_in.at[s, ks, :], g_sem.at[s, k])

    def o_copy(c):
        cs = pl.ds(pl.multiple_of((c % per) * COLS, COLS), COLS)
        return pltpu.make_async_copy(res.at[c], o_ref.at[c // per, :, cs], o_sem.at[c])

    def half_rows(which):
        return pl.ds(pl.multiple_of(which * half, half), half)

    def shard(z, part=None):
        z = lax.rem(z + chips, chips)
        n = rows if part is None else rows // 2
        return pl.ds(pl.multiple_of(z * rows + (0 if part is None else part * n), n), n)

    def res_rows(z, c, part=None):
        z = lax.rem(z + chips, chips)
        n = rows if part is None else rows // 2
        return pl.ds(pl.multiple_of(c * half + z * rows + (0 if part is None else part * n), n), n)

    h = rows // 2

    def x_copy(c):
        return remote(x_tx.at[c], x_rx.at[c], x_send.at[c], x_recv.at[c], partner)

    def r_copy(c, way, s):
        n = h if s == 0 else rows
        return remote(r_tx.at[c, way, s, pl.ds(0, n), :], r_rx.at[c, way, s, pl.ds(0, n), :],
                      r_send.at[c, way], r_recv.at[c, way, s], ahead[way])

    def q_copy(c, way, s):
        rs = res_rows(chip - sign[way] * s, core, way if s == hops - 1 else None)
        return remote(res.at[c, rs, :], res.at[c, rs, :], q_send.at[c, way], q_recv.at[c, way, s], ahead[way])

    def f_copy(c, rs):
        return remote(res.at[c, rs, :], res.at[c, rs, :], f_send.at[c], f_recv.at[c], partner)

    def stage_exchange(c):
        x_copy(c).wait_recv()
        own[c] = own[c] + x_rx[c].astype(F32)
        for way in range(2):
            r_tx[c, way, 0, pl.ds(0, h), :] = own[c, shard(chip + hops, way), :].astype(BF16)
            r_copy(c, way, 0).start()

    def stage_reduce(s):
        def run(c):
            for way in range(2):
                r_copy(c, way, s - 1).wait_recv()
                z = chip + sign[way] * (hops - s)
                if s == 1:
                    r_tx[c, way, s, pl.ds(way * h, h), :] = (
                        own[c, shard(z, way), :] + r_rx[c, way, 0, pl.ds(0, h), :].astype(F32)).astype(BF16)
                    r_tx[c, way, s, pl.ds((1 - way) * h, h), :] = own[c, shard(z, 1 - way), :].astype(BF16)
                else:
                    r_tx[c, way, s] = (own[c, shard(z), :] + r_rx[c, way, s - 1].astype(F32)).astype(BF16)
                r_copy(c, way, s).start()
        return run

    def stage_finish(c):
        for way in range(2):
            r_copy(c, way, hops - 1).wait_recv()
        total = own[c, shard(chip), :] + r_rx[c, 0, hops - 1].astype(F32) + r_rx[c, 1, hops - 1].astype(F32)
        res[c, res_rows(chip, core), :] = total.astype(BF16)
        for way in range(2):
            q_copy(c, way, 0).start()
        f_copy(c, res_rows(chip, core)).start()

    def stage_gather(s):
        def run(c):
            for way in range(2):
                rs = res_rows(chip - sign[way] * s, core, way if s == hops else None)
                remote(res.at[c, rs, :], res.at[c, rs, :], q_send.at[c, way], q_recv.at[c, way, s - 1],
                       ahead[way]).wait_recv()
                if s < hops:
                    q_copy(c, way, s).start()
                f_copy(c, rs).start()
        return run

    def stage_out(c):
        f_copy(c, half_rows(1 - core)).wait_recv()
        o_copy(c).start()

    stages = [stage_exchange, *[stage_reduce(s) for s in range(1, hops)], stage_finish,
              *[stage_gather(s) for s in range(1, hops + 1)], stage_out]

    def piece(c):
        n, j = c // per, lax.rem(c, per)
        s = lax.rem(c, DEPTH)

        @pl.when(c + DEPTH - 1 < pieces)
        def _():
            each(0, steps, lambda k: g_copy(c + DEPTH - 1, k).start())

        @pl.when(j == 0)
        def _():
            def step(k):
                a_copy(n, k).wait()
                g_copy(c, k).wait()
                ks = pl.ds(pl.multiple_of(k * TOKS, TOKS), TOKS)
                t = a_in[ks, :].T
                a_t[:, ks] = t
                part = jnp.dot(t, g_in[s, ks, :], preferred_element_type=F32)

                @pl.when(k == 0)
                def _():
                    acc[...] = part

                @pl.when(k > 0)
                def _():
                    acc[...] += part
            each(0, steps, step)

        @pl.when(j > 0)
        def _():
            each(0, steps, lambda k: g_copy(c, k).wait())

            @pl.when((j == 1) & (n + 1 < mats))
            def _():
                each(0, steps, lambda k: a_copy(n + 1, k).start())
            acc[...] = jnp.dot(a_t[...], g_in[s], preferred_element_type=F32)

        x_tx[c] = acc[half_rows(1 - core), :].astype(BF16)
        x_copy(c).start()
        own[c] = acc[half_rows(core), :]

    def first(k):
        a_copy(0, k).start()
        g_copy(0, k).start()
    each(0, steps, first)
    for c in range(1, DEPTH - 1):
        each(0, steps, lambda k: g_copy(c, k).start())

    def tick(t):
        @pl.when(t < pieces)
        def _():
            piece(t)
        for i, stage in enumerate(stages):
            c = t - 1 - LAG * i

            @pl.when((c >= 0) & (c < pieces))
            def _(stage=stage, c=c):
                stage(c)
    each(0, pieces + 1 + LAG * (len(stages) - 1), tick)

    sent = (2 * hops - 1) * h

    def drain(c):
        x_copy(c).wait_send()
        for way in range(2):
            part = x_tx.at[c, pl.ds(0, sent), :]
            remote(part, part, r_send.at[c, way], r_recv.at[c, way, 0], ahead[way]).wait_send()
            remote(part, part, q_send.at[c, way], q_recv.at[c, way, 0], ahead[way]).wait_send()
        f_copy(c, half_rows(core)).wait_send()
        o_copy(c).wait()
    each(0, pieces, drain)


def solution(mesh):
    chips = mesh.shape["dp"] // 2
    spec = jax.sharding.PartitionSpec

    def local(a, g):
        a, g = a[0], g[0]
        mats, toks, d = a.shape
        ff = g.shape[2]
        pieces, steps = mats * (ff // COLS), toks // TOKS
        half, rows, hops = d // 2, d // 2 // chips, chips // 2
        dma = pltpu.SemaphoreType.DMA
        return pl.pallas_call(
            functools.partial(sums_kernel, chips),
            out_shape=jax.ShapeDtypeStruct((mats, d, ff), BF16),
            in_specs=[pl.BlockSpec(memory_space=pl.ANY)] * 2,
            out_specs=pl.BlockSpec(memory_space=pl.ANY),
            scratch_shapes=[
                pltpu.VMEM((toks, d), BF16),
                pltpu.VMEM((d, toks), BF16),
                pltpu.VMEM((DEPTH, toks, COLS), BF16),
                pltpu.VMEM((d, COLS), F32),
                pltpu.VMEM((pieces, half, COLS), F32),
                pltpu.VMEM((pieces, half, COLS), BF16),
                pltpu.VMEM((pieces, half, COLS), BF16),
                pltpu.VMEM((pieces, 2, hops, rows, COLS), BF16),
                pltpu.VMEM((pieces, 2, hops, rows, COLS), BF16),
                pltpu.VMEM((pieces, d, COLS), BF16),
                dma((steps,)), dma((DEPTH, steps)), dma((pieces,)),
                dma((pieces,)), dma((pieces,)),
                dma((pieces, 2)), dma((pieces, 2, hops)),
                dma((pieces, 2)), dma((pieces, 2, hops)),
                dma((pieces,)), dma((pieces,)),
            ],
            compiler_params=pltpu.CompilerParams(
                collective_id=0, has_side_effects=True, vmem_limit_bytes=63 * 2**20),
            cost_estimate=pl.CostEstimate(
                flops=2 * mats * toks * d * ff, transcendentals=0,
                bytes_accessed=2 * mats * (toks * (d + ff) + d * ff)),
            name="sums",
        )(a, g)

    return jax.shard_map(local, mesh=mesh, in_specs=(spec(("rep", "dp")), spec(("rep", "dp"))),
                         out_specs=spec("rep"), check_vma=False)
```

time: 182 us -> 114 us (0.63)
  blocking collectives: 125 us -> 0 us
  Pallas kernels: 0 us -> 109 us
  matrix products: 55.4 us -> 0 us
  local copies, waits for them, and re-layouts: 0 us -> 5.18 us
    dot_general x1 -> x0, blocking collectives: 125 us -> none  [step(): jnp.einsum('rsntd,rsntf->rndf', a, g, preferred_element_type=jnp.float32)]
    pallas_call x0 -> x1, Pallas kernels: none -> 109 us  [local(): pl.pallas_call(functools.partial(sums_kernel, chips), out_shape=jax.Shape...]
    dot_general x1 -> x0, matrix products: 55.4 us -> none  [step(): jnp.einsum('rsntd,rsntf->rndf', a, g, preferred_element_type=jnp.float32)]
    unnamed x0 -> x1, local copies, waits for them, and re-layouts: none -> 5.18 us
where the time goes in v1:
time: 114 us
  Pallas kernels  109 us (96%)
  local copies, waits for them, and re-layouts  5.18 us (5%)
    pallas_call x1, Pallas kernels, local(): pl.pallas_call(functools.partial(sums_kernel, chips), out_shape=jax.Shape...  109 us
    unnamed x1, local copies, waits for them, and re-layouts  5.18 us

profile of v1, /device:TPU:21, one launch (start us, length us, event | category | flops | bytes accessed | tf_op | source)
XLA Modules:
  0.0 113.7 jit_solution(2791978350860662666)
XLA Ops:
  0.0 108.5 %sums.1 = bf16[4,512,1280]{2,1,0:T(8,128)(2,1)} custom-call(bf16[4,8192,512]{2,1,0:T(8,128)(2,1)} %bitcast.2, bf16[4,8192,1280]{2,1,0:T(8,128)(2,1)} %bitcast.1.g_ref), custom_call_target="tpu_custom_call" | custom-call | flops 42949672960 | bytes 122683392 | tf_op jit(solution)/shard_map/sums/pallas_call | solution.py:226
  108.6 5.2 %copy.4 = bf16[4,512,1280]{2,1,0:T(8,128)(2,1)} copy(bf16[4,512,1280]{2,1,0:T(8,128)(2,1)} %sums.1) | data formatting | bytes 10485760

commit v2 on v1

v2 whole, which is shorter than its diff:
```python
import functools

import jax
import jax.numpy as jnp
from jax import lax
from jax.experimental import pallas as pl
from jax.experimental.pallas import tpu as pltpu

BF16, F32 = jnp.bfloat16, jnp.float32
COLS = 256
TOKS = 2048
DEPTH = 3
SUM_LAG = 3
SHARE_LAG = 3


def sums_kernel(chips, a_ref, g_ref, res, a_in, a_t, g_in, acc, own, x_tx, x_rx, r_tx, r_rx,
                a_sem, g_sem, x_send, x_recv, r_send, r_recv, q_send, q_recv, f_send, f_recv):
    mats, toks, d = a_ref.shape
    per = g_ref.shape[2] // COLS
    steps = toks // TOKS
    pieces = mats * per
    half = d // 2
    rows = half // chips
    hops = chips // 2
    mid = hops // 2

    rep, me = lax.axis_index("rep"), lax.axis_index("dp")
    chip, core = me // 2, lax.rem(me, 2)

    def at(z, c):
        return (rep, lax.rem(z + chips, chips) * 2 + c)

    partner, up, down = at(chip, 1 - core), at(chip + 1, core), at(chip - 1, core)
    ahead = (up, down)
    sign = (1, -1)

    def remote(src, dst, ss, rs, dev):
        return pltpu.make_async_remote_copy(src_ref=src, dst_ref=dst, send_sem=ss, recv_sem=rs, device_id=dev,
                                            device_id_type=pl.DeviceIdType.MESH)

    def each(lo, hi, f):
        def body(i, carry):
            f(i)
            return carry
        lax.fori_loop(lo, hi, body, 0)

    def a_copy(n, k):
        ks = pl.ds(pl.multiple_of(k * TOKS, TOKS), TOKS)
        return pltpu.make_async_copy(a_ref.at[n, ks, :], a_in.at[ks, :], a_sem.at[k])

    def g_copy(c, k):
        ks = pl.ds(pl.multiple_of(k * TOKS, TOKS), TOKS)
        cs = pl.ds(pl.multiple_of((c % per) * COLS, COLS), COLS)
        s = lax.rem(c, DEPTH)
        return pltpu.make_async_copy(g_ref.at[c // per, ks, cs], g_in.at[s, ks, :], g_sem.at[s, k])

    def done(c, rs):
        cs = pl.ds(pl.multiple_of((c % per) * COLS, COLS), COLS)
        return res.at[c // per, rs, cs]

    def half_rows(which):
        return pl.ds(pl.multiple_of(which * half, half), half)

    def shard(z, part=None):
        z = lax.rem(z + chips, chips)
        n = rows if part is None else rows // 2
        return pl.ds(pl.multiple_of(z * rows + (0 if part is None else part * n), n), n)

    def res_rows(z, c, part=None):
        z = lax.rem(z + chips, chips)
        n = rows if part is None else rows // 2
        return pl.ds(pl.multiple_of(c * half + z * rows + (0 if part is None else part * n), n), n)

    h = rows // 2

    def landed(sem, n):
        part = x_rx.at[0, pl.ds(0, n), :]
        remote(part, part, x_send.at[0], sem, partner).wait_recv()

    def x_copy(c):
        return remote(x_tx.at[c], x_rx.at[c], x_send.at[c], x_recv.at[c], partner)

    def r_copy(c, way, s):
        n = h if s == 0 else rows
        return remote(r_tx.at[c, way, s, pl.ds(0, n), :], r_rx.at[c, way, s, pl.ds(0, n), :],
                      r_send.at[c], r_recv.at[c, s], ahead[way])

    def q_copy(c, way, gap, ahead_by):
        far = gap + ahead_by
        rs = res_rows(chip - sign[way] * gap, core, way if far == hops else None)
        return remote(done(c, rs), done(c, rs), q_send.at[c], q_recv.at[c, 1 if far == mid else 0],
                      at(chip + sign[way] * ahead_by, core))

    def f_copy(c, rs):
        return remote(done(c, rs), done(c, rs), f_send.at[c], f_recv.at[c], partner)

    def stage_exchange(c):
        x_copy(c).wait_recv()
        own[c] = own[c] + x_rx[c].astype(F32)
        for way in range(2):
            r_tx[c, way, 0, pl.ds(0, h), :] = own[c, shard(chip + hops, way), :].astype(BF16)
            r_copy(c, way, 0).start()

    def stage_reduce(s):
        def run(c):
            landed(r_recv.at[c, s - 1], 2 * (h if s == 1 else rows))
            for way in range(2):
                z = chip + sign[way] * (hops - s)
                if s == 1:
                    r_tx[c, way, s, pl.ds(way * h, h), :] = (
                        own[c, shard(z, way), :] + r_rx[c, way, 0, pl.ds(0, h), :].astype(F32)).astype(BF16)
                    r_tx[c, way, s, pl.ds((1 - way) * h, h), :] = own[c, shard(z, 1 - way), :].astype(BF16)
                else:
                    r_tx[c, way, s] = (own[c, shard(z), :] + r_rx[c, way, s - 1].astype(F32)).astype(BF16)
                r_copy(c, way, s).start()
        return run

    def stage_finish(c):
        landed(r_recv.at[c, hops - 1], 2 * rows)
        total = own[c, shard(chip), :] + r_rx[c, 0, hops - 1].astype(F32) + r_rx[c, 1, hops - 1].astype(F32)
        done(c, res_rows(chip, core))[...] = total.astype(BF16)
        for d in range(mid, 0, -1):
            for way in range(2):
                q_copy(c, way, 0, d).start()

    def stage_forward(c):
        landed(q_recv.at[c, 1], 2 * rows)
        for way in range(2):
            for d in range(hops - mid, 0, -1):
                q_copy(c, way, mid, d).start()

    def stage_settle(c):
        landed(q_recv.at[c, 0], half - 3 * rows)
        f_copy(c, half_rows(core)).start()

    def stage_out(c):
        f_copy(c, half_rows(1 - core)).wait_recv()

    stages = [(stage_exchange, 2)]
    for s in range(1, hops):
        stages.append((stage_reduce(s), stages[-1][1] + SUM_LAG))
    stages.append((stage_finish, stages[-1][1] + SUM_LAG))
    stages.append((stage_forward, stages[-1][1] + SHARE_LAG))
    stages.append((stage_settle, stages[-1][1] + SHARE_LAG))
    stages.append((stage_out, stages[-1][1] + 2))
    ticks = pieces + stages[-1][1] // 2

    def run(phase, t):
        for stage, place in stages[1:] + stages[:1]:
            if place % 2 != phase:
                continue
            c = t - place // 2

            @pl.when((c >= 0) & (c < pieces))
            def _(stage=stage, c=c):
                stage(c)

    def fetch(c):
        @pl.when(c + DEPTH - 1 < pieces)
        def _():
            each(0, steps, lambda k: g_copy(c + DEPTH - 1, k).start())

    def piece_first(c, lo, hi):
        n, s = c // per, lax.rem(c, DEPTH)

        def step(k):
            a_copy(n, k).wait()
            g_copy(c, k).wait()
            ks = pl.ds(pl.multiple_of(k * TOKS, TOKS), TOKS)
            t = a_in[ks, :].T
            a_t[:, ks] = t
            part = jnp.dot(t, g_in[s, ks, :], preferred_element_type=F32)

            @pl.when(k == 0)
            def _():
                acc[...] = part

            @pl.when(k > 0)
            def _():
                acc[...] += part
        each(lo, hi, step)

    def first_terms(c):
        x_tx[c] = acc[half_rows(1 - core), :].astype(BF16)
        x_copy(c).start()
        own[c] = acc[half_rows(core), :]

    def piece_other(c):
        n, j, s = c // per, lax.rem(c, per), lax.rem(c, DEPTH)
        each(0, steps, lambda k: g_copy(c, k).wait())

        @pl.when((j == 1) & (n + 1 < mats))
        def _():
            each(0, steps, lambda k: a_copy(n + 1, k).start())
        x_tx[c] = jnp.dot(a_t[half_rows(1 - core), :], g_in[s], preferred_element_type=F32).astype(BF16)
        x_copy(c).start()

    def piece_own(c):
        s = lax.rem(c, DEPTH)
        own[c] = jnp.dot(a_t[half_rows(core), :], g_in[s], preferred_element_type=F32)

    barrier = pltpu.get_barrier_semaphore()
    others = [partner, *[at(chip + w * k, core) for k in range(1, mid + 1) for w in sign]]
    for dev in others:
        pl.semaphore_signal(barrier, inc=1, device_id=dev, device_id_type=pl.DeviceIdType.MESH)

    def first(k):
        a_copy(0, k).start()
        g_copy(0, k).start()
    each(0, steps, first)
    piece_first(0, 0, steps // 2)
    for c in range(1, DEPTH - 1):
        each(0, steps, lambda k: g_copy(c, k).start())
    piece_first(0, steps // 2, steps)
    fetch(0)
    pl.semaphore_wait(barrier, len(others))
    first_terms(0)

    def tick(t):
        more = t < pieces
        later = more & (lax.rem(t, per) > 0)
        newer = more & (lax.rem(t, per) == 0)

        @pl.when(more)
        def _():
            fetch(t)

        @pl.when(newer)
        def _():
            piece_first(t, 0, steps // 2)

        @pl.when(later)
        def _():
            piece_other(t)
        run(0, t)

        @pl.when(newer)
        def _():
            piece_first(t, steps // 2, steps)
            first_terms(t)

        @pl.when(later)
        def _():
            piece_own(t)
        run(1, t)
    each(1, ticks, tick)

    def drain(c):
        x_copy(c).wait_send()
        part = x_tx.at[c, pl.ds(0, half - rows), :]
        remote(part, part, r_send.at[c], r_recv.at[c, 0], partner).wait_send()
        remote(part, part, q_send.at[c], q_recv.at[c, 0], partner).wait_send()
        f_copy(c, half_rows(core)).wait_send()
    each(0, pieces, drain)


def solution(mesh):
    chips = mesh.shape["dp"] // 2
    spec = jax.sharding.PartitionSpec

    def local(a, g):
        a, g = a[0], g[0]
        mats, toks, d = a.shape
        ff = g.shape[2]
        pieces, steps = mats * (ff // COLS), toks // TOKS
        half, rows, hops = d // 2, d // 2 // chips, chips // 2
        dma = pltpu.SemaphoreType.DMA
        return pl.pallas_call(
            functools.partial(sums_kernel, chips),
            out_shape=pltpu.VMEM((mats, d, ff), BF16),
            in_specs=[pl.BlockSpec(memory_space=pl.ANY)] * 2,
            out_specs=pl.BlockSpec(memory_space=pltpu.VMEM),
            scratch_shapes=[
                pltpu.VMEM((toks, d), BF16),
                pltpu.VMEM((d, toks), BF16),
                pltpu.VMEM((DEPTH, toks, COLS), BF16),
                pltpu.VMEM((d, COLS), F32),
                pltpu.VMEM((pieces, half, COLS), F32),
                pltpu.VMEM((pieces, half, COLS), BF16),
                pltpu.VMEM((pieces, half, COLS), BF16),
                pltpu.VMEM((pieces, 2, hops, rows, COLS), BF16),
                pltpu.VMEM((pieces, 2, hops, rows, COLS), BF16),
                dma((steps,)), dma((DEPTH, steps)),
                dma((pieces,)), dma((pieces,)),
                dma((pieces,)), dma((pieces, hops)),
                dma((pieces,)), dma((pieces, 2)),
                dma((pieces,)), dma((pieces,)),
            ],
            compiler_params=pltpu.CompilerParams(
                collective_id=0, has_side_effects=True, vmem_limit_bytes=52 * 2**20),
            cost_estimate=pl.CostEstimate(
                flops=2 * mats * toks * d * ff, transcendentals=0,
                bytes_accessed=2 * mats * (toks * (d + ff) + d * ff)),
            name="sums",
        )(a, g)

    return jax.shard_map(local, mesh=mesh, in_specs=(spec(("rep", "dp")), spec(("rep", "dp"))),
                         out_specs=spec("rep"), check_vma=False)
```

time: 114 us -> 104 us (0.912)
  Pallas kernels: 109 us -> 101 us
  local copies, waits for them, and re-layouts: 5.18 us -> 2.36 us
    pallas_call x1, Pallas kernels: 109 us -> 101 us  [local(): pl.pallas_call(functools.partial(sums_kernel, chips), out_shape=pltpu.VME...]
    unnamed x1, local copies, waits for them, and re-layouts: 5.18 us -> 2.36 us
where the time goes in v2:
time: 104 us
  Pallas kernels  101 us (97%)
  local copies, waits for them, and re-layouts  2.36 us (2%)
    pallas_call x1, Pallas kernels, local(): pl.pallas_call(functools.partial(sums_kernel, chips), out_shape=pltpu.VME...  101 us
    unnamed x1, local copies, waits for them, and re-layouts  2.36 us

profile of v2, /device:TPU:21, one launch (start us, length us, event | category | flops | bytes accessed | tf_op | source)
XLA Modules:
  0.0 103.6 jit_solution(6533258865395271919)
XLA Ops:
  0.0 101.3 %sums.1 = bf16[4,512,1280]{2,1,0:T(8,128)(2,1)S(1)} custom-call(bf16[4,8192,512]{2,1,0:T(8,128)(2,1)} %bitcast.2, bf16[4,8192,1280]{2,1,0:T(8,128)(2,1)} %bitcast.1.g_ref), custom_call_target="tpu_custom_call" | custom-call | flops 42949672960 | bytes 122683392 | tf_op jit(solution)/shard_map/sums/pallas_call | solution.py:269
  101.3 2.4 %copy.4 = bf16[4,512,1280]{2,1,0:T(8,128)(2,1)} copy(bf16[4,512,1280]{2,1,0:T(8,128)(2,1)S(1)} %sums.1) | data formatting | bytes 10485760

commit v3 on v2

--- a/solution.py
+++ b/solution.py
@@ -8,7 +8,7 @@
 
 BF16, F32 = jnp.bfloat16, jnp.float32
 COLS = 256
-TOKS = 2048
+TOKS = 4096
 DEPTH = 3
 SUM_LAG = 3
 SHARE_LAG = 3

time: 104 us -> 102 us (0.981)
    pallas_call x1, Pallas kernels: 101 us -> 100 us  [local(): pl.pallas_call(functools.partial(sums_kernel, chips), out_shape=pltpu.VME...]
where the time goes in v3:
time: 102 us
  Pallas kernels  100 us (98%)
  local copies, waits for them, and re-layouts  2.36 us (2%)
    pallas_call x1, Pallas kernels, local(): pl.pallas_call(functools.partial(sums_kernel, chips), out_shape=pltpu.VME...  100 us
    unnamed x1, local copies, waits for them, and re-layouts  2.36 us

profile of v3, /device:TPU:21, one launch (start us, length us, event | category | flops | bytes accessed | tf_op | source)
XLA Modules:
  0.0 102.3 jit_solution(17832150399488507644)
XLA Ops:
  0.0 100.0 %sums.1 = bf16[4,512,1280]{2,1,0:T(8,128)(2,1)S(1)} custom-call(bf16[4,8192,512]{2,1,0:T(8,128)(2,1)} %bitcast.2, bf16[4,8192,1280]{2,1,0:T(8,128)(2,1)} %bitcast.1.g_ref), custom_call_target="tpu_custom_call" | custom-call | flops 42949672960 | bytes 122683392 | tf_op jit(solution)/shard_map/sums/pallas_call | solution.py:269
  100.0 2.4 %copy.4 = bf16[4,512,1280]{2,1,0:T(8,128)(2,1)} copy(bf16[4,512,1280]{2,1,0:T(8,128)(2,1)S(1)} %sums.1) | data formatting | bytes 10485760
